TPU v7x, 512 devices: a whole 4x4x16 slice. The times are simulated.
512 devices in a mesh: segment: 16 (over z_hi, y, core), dp: 32 (over x, z_lo).
Axes of the slice: x: 4, y: 4, z: 16 (z_hi: 2, z_lo: 8; z = z_hi * 8 + z_lo), core: 2. Of those that a mesh axis runs over, the one named last changes fastest.
Arguments:
- token_ids: int32 [4096], P('dp'), may hold values from 0 to 152063, as said below
- table: bfloat16 [19008, 28672], P('segment', 'dp'), may hold values from -6 to 6
- out_grad: bfloat16 [4096, 3584], P('dp', 'segment'), may hold values from -6 to 6
Outputs:
- embedded: bfloat16 [4096, 3584], P('dp')
- table_grad: bfloat16 [19008, 28672], P('segment', 'dp')
Inputs may be any that keep to these rules, and one draw needn't show every extreme that they name: `token_ids`: in the 128 tokens of each data group, at most 16 ids lie in one segment's slice of 9504 rows with one residue modulo 8; in every data group some segment and residue has exactly 16.
All inputs are finite; a program needn't handle non-finite values.
Results may differ from a plain program's by a relative error of at most 0.001.
Values may be sent and summed in bfloat16 or wider, within the bound.
No kernel may reach another device: no remote copies, remote signals or barrier semaphores. Data moves between devices by JAX's collectives and lax.ppermute only.
A program may use at most 64 MiB of HBM per device.

v0:
```python
import jax
import jax.numpy as jnp
from jax import lax
from jax.sharding import PartitionSpec as P

D = 3584
PACK = 8


def copy_for_each(shard, axis):
    size = lax.axis_size(axis)
    return lax.all_to_all(
        jnp.broadcast_to(shard[None], (size, *shard.shape)), axis, 0, 0, tiled=True
    )


def joined_along(tiles, dim):
    tiles = jnp.moveaxis(tiles, 0, dim)
    shape = tiles.shape
    return tiles.reshape(*shape[:dim], shape[dim] * shape[dim + 1], *shape[dim + 2 :])


def collect(shard, axis, dim):
    tiles = copy_for_each(shard, axis)
    return joined_along(tiles, dim)


def filled_up(lines, size):
    spare = -lines.shape[0] % size
    if not spare:
        return lines
    return jnp.concatenate([lines, jnp.zeros((spare, *lines.shape[1:]), lines.dtype)])


def sum_in_two_steps(shard, axis):
    lines = shard.reshape(-1, *shard.shape[1:][-1:])
    padded = filled_up(lines, lax.axis_size(axis))
    own = lax.psum_scatter(padded, axis, scatter_dimension=0, tiled=True)
    whole = lax.all_gather(own, axis, axis=0, tiled=True)
    return whole[: len(lines)].reshape(shard.shape)


def body(token_ids, table, out_grad):
    lines = table.shape[0]
    width = table.shape[1]
    groups = lax.axis_size("dp")
    tok_rows = token_ids.shape[0]
    quarters = D // width
    slot = lax.axis_index("dp") // quarters
    first = lax.axis_index("segment") * lines * PACK
    every_id = collect(token_ids, "dp", 0)
    local = every_id - first
    in_section = (local >= 0) & (local < lines * PACK)
    owned = in_section & (local % PACK == slot)
    line_idx = jnp.clip(local // PACK, 0, lines - 1)
    whole_grad = lax.all_gather(out_grad, "segment", axis=1, tiled=True)
    capacity = tok_rows // PACK
    owned_grid = owned.reshape(groups, tok_rows)
    rank = jnp.cumsum(owned_grid.astype(jnp.int32), axis=1) - 1
    place = jnp.where(owned_grid, rank, capacity)
    group_rows = jnp.broadcast_to(jnp.arange(groups, dtype=jnp.int32)[:, None], (groups, tok_rows))
    row_of = (
        jnp.zeros((groups, capacity), jnp.int32)
        .at[group_rows, place]
        .set(line_idx.reshape(groups, tok_rows), mode="drop")
    )
    filled = jnp.zeros((groups, capacity), jnp.bool_).at[group_rows, place].set(True, mode="drop")
    fetched = jnp.take(table, row_of.reshape(-1), axis=0).reshape(groups, capacity, width)
    fetched = jnp.where(filled[:, :, None], fetched, jnp.zeros((), jnp.bfloat16))
    arrived = lax.all_to_all(fetched, "dp", split_axis=0, concat_axis=0, tiled=True)
    my_local = token_ids - first
    my_in = (my_local >= 0) & (my_local < lines * PACK)
    my_slot = my_local % PACK
    slot_hits = (my_slot[:, None] == jnp.arange(PACK, dtype=jnp.int32)[None, :]) & my_in[:, None]
    slot_ranks = jnp.cumsum(slot_hits.astype(jnp.int32), axis=0) - 1
    my_rank = jnp.sum(jnp.where(slot_hits, slot_ranks, 0), axis=1)
    sources = my_slot[:, None] * quarters + jnp.arange(quarters, dtype=jnp.int32)[None, :]
    flat_index = jnp.clip(sources * capacity + my_rank[:, None], 0, groups * capacity - 1)
    gathered = jnp.take(
        arrived.reshape(groups * capacity, width), flat_index.reshape(-1), axis=0
    ).reshape(tok_rows, D)
    segment_part = jnp.where(my_in[:, None], gathered.astype(jnp.float32), 0.0)
    slot_place = jnp.where(my_in, my_slot, PACK)
    token_at = (
        jnp.zeros((PACK, capacity), jnp.int32)
        .at[slot_place, my_rank]
        .set(jnp.arange(tok_rows, dtype=jnp.int32), mode="drop")
    )
    valid = jnp.zeros((PACK, capacity), jnp.bool_).at[slot_place, my_rank].set(True, mode="drop")
    grad_pick = jnp.take(whole_grad, token_at.reshape(-1), axis=0).reshape(
        PACK, capacity, quarters, width
    )
    grad_pick = jnp.where(valid[:, :, None, None], grad_pick, jnp.zeros((), jnp.bfloat16))
    grad_send = grad_pick.transpose(0, 2, 1, 3).reshape(groups, capacity, width)
    returned = lax.all_to_all(grad_send, "dp", split_axis=0, concat_axis=0, tiled=True)
    target = jnp.where(filled, row_of, lines)
    accum = (
        jnp.zeros((lines, width), jnp.float32)
        .at[target.reshape(-1)]
        .add(returned.reshape(-1, width).astype(jnp.float32), mode="drop")
    )
    embedded = (
        sum_in_two_steps(segment_part.astype(jnp.bfloat16), "segment")
        .astype(jnp.float32)
        .astype(jnp.bfloat16)
    )
    return (embedded, accum.astype(jnp.bfloat16))


def solution(mesh):
    placed = (P("dp"), P("segment", "dp"), P("dp", "segment"))
    return jax.shard_map(
        body,
        mesh=mesh,
        in_specs=placed,
        out_specs=(P("dp", None), P("segment", "dp")),
        check_vma=False,
    )
```

profile of v0, /device:TPU:1, one launch (start us, length us, event | category | flops | bytes accessed | tf_op | source)
XLA Modules:
  0.0 367.0 jit_solution(8499920811396235449)
XLA Ops:
  7.2 1.4 broadcast_in_dim.139
  8.6 15.9 %all-to-all-start = ((s32[32,1,128]{2,1,0:T(1,128)}), s32[32,1,128]{2,1,0:T(1,128)S(1)}, u32[]{:S(2)}, u32[]{:S(2)}) async-start(s32[32,1,128]{2,1,0:T(1,128)} %broadcast_in_dim.139), calls=%async_computation | async-start | bytes 32768 | tf_op jit(solution)/shard_map/all_to_all | solution.py:12
  24.5 11.3 %all-to-all-done = s32[32,1,128]{2,1,0:T(1,128)S(1)} async-done(((s32[32,1,128]{2,1,0:T(1,128)}), s32[32,1,128]{2,1,0:T(1,128)S(1)}, u32[]{:S(2)}, u32[]{:S(2)}) %all-to-all-start) | async-done | bytes 16416 | tf_op jit(solution)/shard_map/all_to_all | solution.py:12
  35.8 2.9 copy.38
  38.7 4.9 %broadcast_compare_fusion = (pred[32,128,1]{2,0,1:T(8,128)(4,1)S(1)}, s32[32,128,1]{2,0,1:T(8,128)S(1)}) fusion(s32[32,128,1]{2,0,1:T(8,128)} %copy.38, s32[]{:T(128)S(6)} %select_n.177), kind=kOutput, calls=%fused_computation.27 | output fusion | flops 667648 | bytes 36868 | tf_op jit(solution)/shard_map/jit(cumsum)/reduce_window_sum | solution.py:59
  43.6 1.3 copy-done.1
  44.9 1.6 broadcast_add_fusion
  46.5 2.7 copy.45
  49.2 2.7 copy.44
  51.8 1.5 copy.43
  53.5 15.7 %scatter_custom_fusion.4 = s32[512]{0:T(512)S(1)} fusion(s32[4096]{0:T(1024)S(1)} %get-tuple-element.7, s32[4096]{0:T(1024)S(1)} %get-tuple-element.6, s32[]{:T(128)} %constant.87.clone.1), kind=kCustom, calls=%fused_computation.73 | custom fusion | bytes 2052
  69.3 17.6 %scatter_custom_fusion.3 = pred[512]{0:T(512)(128)(4,1)S(1)} fusion(s32[4096]{0:T(1024)S(1)} %get-tuple-element.7, pred[4096]{0:T(1024)(128)(4,1)S(1)} %broadcast.426, pred[]{:T(512)} %constant.135.clone.1), kind=kCustom, calls=%fused_computation.75 | custom fusion | bytes 513
  87.4 2.1 gather_fusion
  89.4 1.2 select_select_fusion
  90.6 3.9 %all-to-all-start.1 = ((bf16[32,16,896]{2,1,0:T(8,128)(2,1)}), bf16[32,16,896]{2,1,0:T(8,128)(2,1)S(1)}, u32[]{:S(2)}, u32[]{:S(2)}) async-start(bf16[32,16,896]{2,1,0:T(8,128)(2,1)} %select_select_fusion), calls=%async_computation.1 | async-start | bytes 1835008 | tf_op jit(solution)/shard_map/all_to_all | solution.py:70
  95.1 6.4 %scatter_fusion.1 = s32[8,16]{1,0:T(8,128)S(1)} fusion(s32[8,16]{1,0:T(8,128)S(1)} %broadcast_in_dim.154, s32[128]{0:T(128)S(1)} %fusion.32, s32[128]{0:T(128)S(1)} %iota.18), kind=kCustom, calls=%fused_computation.4 | custom fusion | bytes 2560 | tf_op jit(solution)/shard_map/scatter | solution.py:87
  101.6 48.8 %all_gather.7 = bf16[128,3584]{0,1:T(8,128)(2,1)} all-gather(bf16[128,224]{0,1:T(8,128)(2,1)S(1)} %copy-done.2), channel_id=1, replica_groups=mesh['segment'=16,'dp'=32] {'segment'}, dimensions={1}, use_global_device_ids=true | all-gather | bytes 974848 | tf_op jit(solution)/shard_map/all_gather | solution.py:56
  150.4 2.2 copy.54
  152.6 4.3 %gather_fusion.2 = bf16[128,3584]{1,0:T(8,128)(2,1)} fusion(bf16[128,3584]{1,0:T(8,128)(2,1)} %copy.54, s32[1024]{0:T(1024)S(1)} %pad_clamp_fusion), kind=kCustom, calls=%fused_computation.2 | custom fusion | bytes 1835520 | tf_op jit(solution)/shard_map/jit(_take)/gather | solution.py:90
  156.8 2.7 gather.23
  159.5 6.5 %scatter_fusion = pred[8,16]{1,0:T(8,128)(4,1)S(1)} fusion(pred[8,16]{1,0:T(8,128)(4,1)S(1)} %broadcast_in_dim.150, s32[128]{0:T(128)S(1)} %fusion.32, pred[128]{0:T(512)(128)(4,1)S(1)} %broadcast.427), kind=kCustom, calls=%fused_computation.3 | custom fusion | bytes 1408 | tf_op jit(solution)/shard_map/scatter | solution.py:89
  166.0 2.3 fusion.16
  168.4 37.5 %all-to-all-start.2 = ((bf16[32,16,896]{2,1,0:T(8,128)(2,1)}), bf16[32,16,896]{2,1,0:T(8,128)(2,1)}, u32[]{:S(2)}, u32[]{:S(2)}) async-start(bf16[32,16,896]{2,1,0:T(8,128)(2,1)} %bitcast.56), calls=%async_computation.3 | async-start | bytes 1835008 | tf_op jit(solution)/shard_map/all_to_all | solution.py:95
  207.1 2.7 gather_fusion.1
  209.8 1.7 gather.21
  211.5 1.3 select_convert_fusion
  213.0 38.2 %all-to-all-done.2 = bf16[32,16,896]{2,1,0:T(8,128)(2,1)} async-done(((bf16[32,16,896]{2,1,0:T(8,128)(2,1)}), bf16[32,16,896]{2,1,0:T(8,128)(2,1)}, u32[]{:S(2)}, u32[]{:S(2)}) %all-to-all-start.2) | async-done | bytes 917536 | tf_op jit(solution)/shard_map/all_to_all | solution.py:95
  251.2 7.6 %scatter_custom_fusion.2 = f32[1188,896]{1,0:T(8,128)} fusion(s32[512]{0:T(512)S(1)} %bitcast.65, f32[]{:T(128)} %constant.145.clone.1, bf16[512,896]{1,0:T(8,128)(2,1)} %bitcast.20), kind=kCustom, calls=%fused_computation.11 | custom fusion | flops 917504 | bytes 5175300 | tf_op jit(solution)/shard_map/scatter-add | solution.py:100
  258.8 3.8 %convert_element_type.34 = bf16[1188,896]{1,0:T(8,128)(2,1)} convert(f32[1188,896]{1,0:T(8,128)} %scatter_custom_fusion.2) | non-fusion elementwise | flops 1064448 | bytes 6386688 | tf_op jit(solution)/shard_map/convert_element_type | solution.py:107
  262.5 52.1 %reduce-scatter.2.cloned.1.call-done = bf16[8,3584]{1,0:T(8,128)(2,1)} async-done(((bf16[128,3584]{1,0:T(8,128)(2,1)}), bf16[8,3584]{1,0:T(8,128)(2,1)}) %reduce-scatter.2.cloned.1.call-update) | async-done | bytes 57360 | tf_op jit(solution)/shard_map/reduce_scatter | solution.py:38
  314.6 44.6 %all_gather.6 = bf16[128,3584]{1,0:T(8,128)(2,1)S(1)} all-gather(bf16[8,3584]{1,0:T(8,128)(2,1)} %reduce-scatter.2.cloned.1.call-done), channel_id=1, replica_groups=mesh['segment'=16,'dp'=32] {'segment'}, dimensions={0}, use_global_device_ids=true | all-gather | bytes 974848 | tf_op jit(solution)/shard_map/all_gather | solution.py:39
  359.3 0.9 copy.65
  (55 shorter events, 2.7 us)
Async XLA Ops:
  7.2 80.2 %copy-start = (bf16[1188,896]{1,0:T(8,128)(2,1)S(1)}, bf16[1188,896]{1,0:T(8,128)(2,1)}, u32[]{:S(2)}) copy-start(bf16[1188,896]{1,0:T(8,128)(2,1)} %param.4) | copy-start | bytes 6386692
  8.6 27.2 %all-to-all-start = ((s32[32,1,128]{2,1,0:T(1,128)}), s32[32,1,128]{2,1,0:T(1,128)S(1)}, u32[]{:S(2)}, u32[]{:S(2)}) async-start(s32[32,1,128]{2,1,0:T(1,128)} %broadcast_in_dim.139), calls=%async_computation | async-start | bytes 32768 | tf_op jit(solution)/shard_map/all_to_all | solution.py:12
  43.6 1.4 copy-start.1
  46.5 6.8 %copy-start.5 = (s32[2]{0:T(128)S(1)}, s32[2]{0:T(128)}, u32[]{:S(2)}) copy-start(s32[2]{0:T(128)} %constant.149) | copy-start | bytes 28
  46.5 6.9 %copy-start.4 = (s32[2]{0:T(128)S(1)}, s32[2]{0:T(128)}, u32[]{:S(2)}) copy-start(s32[2]{0:T(128)} %constant.152) | copy-start | bytes 28
  89.4 5.1 %copy-start.3 = (s32[128]{0:T(128)S(1)}, s32[128]{0:T(128)}, u32[]{:S(2)}) copy-start(s32[128]{0:T(128)} %param.3) | copy-start | bytes 1540
  89.4 12.1 %copy-start.2 = (bf16[128,224]{0,1:T(8,128)(2,1)S(1)}, bf16[128,224]{0,1:T(8,128)(2,1)}, u32[]{:S(2)}) copy-start(bf16[128,224]{0,1:T(8,128)(2,1)} %param.5) | copy-start | bytes 172036
  90.6 77.7 %all-to-all-start.1 = ((bf16[32,16,896]{2,1,0:T(8,128)(2,1)}), bf16[32,16,896]{2,1,0:T(8,128)(2,1)S(1)}, u32[]{:S(2)}, u32[]{:S(2)}) async-start(bf16[32,16,896]{2,1,0:T(8,128)(2,1)} %select_select_fusion), calls=%async_computation.1 | async-start | bytes 1835008 | tf_op jit(solution)/shard_map/all_to_all | solution.py:70
  168.4 82.8 %all-to-all-start.2 = ((bf16[32,16,896]{2,1,0:T(8,128)(2,1)}), bf16[32,16,896]{2,1,0:T(8,128)(2,1)}, u32[]{:S(2)}, u32[]{:S(2)}) async-start(bf16[32,16,896]{2,1,0:T(8,128)(2,1)} %bitcast.56), calls=%async_computation.3 | async-start | bytes 1835008 | tf_op jit(solution)/shard_map/all_to_all | solution.py:95
  205.9 108.7 %reduce-scatter.2.cloned.1.call-start = ((), (), s32[]{:S(2)}) async-start(), calls=%async_computation.4 | async-start | bytes 974848 | tf_op jit(solution)/shard_map/reduce_scatter | solution.py:38
Sparse Core Ops, SparseCore 0:
  212.9 101.6 reduce-scatter.1
where the time goes:
time: 368 us; the launch traced here: 367 us
  waiting for transfers between devices  102 us (28%)
  blocking collectives  93.4 us (25%)
  local copies, waits for them, and re-layouts  76.5 us (21%)
  starting transfers between devices  57.6 us (16%)
  other arithmetic  23.6 us (6%)
  between operations  14.3 us (4%)
    reduce_scatter x1, waiting for transfers between devices, sum_in_two_steps(): own = lax.psum_scatter(padded, axis, scatter_dimension=0, tiled=True)  52.1 us
    all_gather x1, blocking collectives, body(): whole_grad = lax.all_gather(out_grad, 'segment', axis=1, tiled=True)  48.8 us
    all_gather x1, blocking collectives, sum_in_two_steps(): whole = lax.all_gather(own, axis, axis=0, tiled=True)  44.6 us
    all_to_all x1, waiting for transfers between devices, body(): lax.all_to_all(grad_send, 'dp', split_axis=0, concat_axis=0, tiled=True)  38.2 us
    all_to_all x1, starting transfers between devices, body(): lax.all_to_all(grad_send, 'dp', split_axis=0, concat_axis=0, tiled=True)  37.5 us
    unnamed x19, local copies, waits for them, and re-layouts  36 us
    all_to_all x1, starting transfers between devices, copy_for_each(): lax.all_to_all(jnp.broadcast_to(shard[None], (size, *shard.shape)), axis,...  15.9 us
    all_to_all x1, waiting for transfers between devices, copy_for_each(): lax.all_to_all(jnp.broadcast_to(shard[None], (size, *shard.shape)), axis,...  11.3 us
  transfers between devices with their start and end apart: 4, of which 3 were waited for; matrix products, arithmetic and copies ran while one was open for 12% of the time, Pallas kernels for 0%

commit v1 on v0

v1 whole, which is shorter than its diff:
```python
import itertools

import jax
import jax.numpy as jnp
from jax import lax
from jax.sharding import Mesh, PartitionSpec as P

D = 3584
PACK = 8
SLOTS = 16
NAMES = ("z_hi", "y", "core", "x", "z_lo")
SIZES = (2, 4, 2, 4, 8)
PLANE = ("y", "core", "x")
GROUPS = ("x", "z_lo")
QUARTERS = 4
WIDTH = D // QUARTERS
BF16 = jnp.bfloat16


def move(values, to):
    def flat(place):
        number = 0
        for size, at in zip(SIZES, place):
            number = number * size + at
        return number

    pairs = [
        (flat(place), flat(to(*place)))
        for place in itertools.product(*(range(size) for size in SIZES))
    ]
    return lax.ppermute(values, NAMES, pairs)


def lookup_code(z_hi, z_lo):
    return z_lo


def grad_code(z_hi, z_lo):
    return z_hi * 4 + (z_lo // 4) * 2 + z_lo % 2


def grad_target(z_hi, y, core, x, z_lo):
    code = (core * 4 + y) ^ z_lo
    return (code // 4, y, core, x, ((code // 2) % 2) * 4 + 2 * z_hi + code % 2)


def groups_of_plane(code):
    at = jnp.arange(32, dtype=jnp.int32)
    y, core, x = at // 8, (at // 4) % 2, at % 4
    return x * 8 + ((core * 4 + y) ^ code)


def pick_matrix(ids, section, z_hi, parity):
    segment = ids // section
    residue = (ids % section) % PACK
    bucket = segment * PACK + residue
    count = ids.shape[0]
    order = jnp.arange(count, dtype=jnp.int32)
    earlier = (bucket[:, None] == bucket[None, :]) & (order[None, :] < order[:, None])
    rank = jnp.sum(earlier.astype(jnp.int32), axis=1)
    here = (segment // 8 == z_hi) & (residue % 2 == parity)
    slot = jnp.where(here, ((segment % 8) * 4 + residue // 2) * SLOTS + rank, -1)
    return (slot[:, None] == jnp.arange(32 * SLOTS, dtype=jnp.int32)[None, :]).astype(BF16)


def body(token_ids, table, out_grad):
    lines, width = table.shape
    section = lines * PACK
    tokens = token_ids.shape[0]
    z_hi, y, core, x, z_lo = (lax.axis_index(name) for name in NAMES)
    segment = (z_hi * 4 + y) * 2 + core
    residue = x * 2 + z_lo // 4
    parity = z_lo // 4
    place = core * 4 + y

    every_id = lax.all_to_all(
        jnp.broadcast_to(token_ids[None], (32, tokens)), GROUPS, 0, 0, tiled=True
    )

    code_f = lookup_code(z_hi, z_lo)
    code_b = grad_code(z_hi, z_lo)
    orders = jnp.concatenate([groups_of_plane(code_f), groups_of_plane(code_b)])
    ids = jnp.take(every_id, orders, axis=0)
    local = ids - segment * section
    owned = (local >= 0) & (local < section) & (local % PACK == residue)
    line = local // PACK
    steps = jnp.arange(tokens, dtype=jnp.int32)
    before = (steps[:, None] < steps[None, :]).astype(BF16)
    rank = jnp.dot(owned.astype(BF16), before, preferred_element_type=jnp.float32).astype(jnp.int32)
    slots = jnp.arange(SLOTS, dtype=jnp.int32)
    hit = owned[:, None, :] & (rank[:, None, :] == slots[None, :, None])
    row_of = jnp.sum(jnp.where(hit, line[:, None, :] + 1, 0), axis=2) - 1

    fetched = jnp.take(table, jnp.maximum(row_of[:32], 0).reshape(-1), axis=0)
    arrived = lax.all_to_all(fetched.reshape(32, SLOTS, width), PLANE, 0, 0, tiled=True)
    ids_f = lax.dynamic_index_in_dim(every_id, x * 8 + (place ^ code_f), 0, keepdims=False)
    pick_f = pick_matrix(ids_f, section, z_hi, parity)
    picked = jnp.dot(
        pick_f, arrived.reshape(32 * SLOTS, width), preferred_element_type=jnp.float32
    ).astype(BF16)

    def near(a, b, c, d, e):
        return (a, b, c, d, e ^ (c * 4 + b))

    def far(a, b, c, d, e):
        return (1 - a, b, c, d, e ^ (c * 4 + b))

    both = move(picked, near) + move(picked, far)
    quarter = both + lax.ppermute(both, "core", [(0, 1), (1, 0)])
    whole = lax.all_gather(quarter, "y")
    embedded = jnp.concatenate(
        [
            lax.dynamic_index_in_dim(whole, (z_lo % 4) ^ part, 0, keepdims=False)
            for part in range(QUARTERS)
        ],
        axis=1,
    )

    halves = lax.all_gather(out_grad, ("y", "core"), axis=1, tiled=True)
    which = (place ^ z_lo) % 2
    piece = lax.dynamic_slice(halves, (0, which * width), (tokens, width))
    piece = move(piece, grad_target)
    ids_b = lax.dynamic_index_in_dim(every_id, x * 8 + (place ^ code_b), 0, keepdims=False)
    pick_b = pick_matrix(ids_b, section, z_hi, parity)
    packed = lax.dot_general(
        pick_b, piece, (((0,), (0,)), ((), ())), preferred_element_type=jnp.float32
    ).astype(BF16)
    returned = lax.all_to_all(packed.reshape(32, SLOTS, width), PLANE, 0, 0, tiled=True)
    target = row_of[32:].reshape(-1)
    spread = (jnp.arange(lines, dtype=jnp.int32)[:, None] == target[None, :]).astype(BF16)
    table_grad = jnp.dot(
        spread, returned.reshape(32 * SLOTS, width), preferred_element_type=jnp.float32
    ).astype(BF16)
    return embedded, table_grad


def solution(mesh):
    fine = Mesh(mesh.devices.reshape(SIZES), NAMES)
    segment, groups = ("z_hi", "y", "core"), ("x", "z_lo")
    return jax.shard_map(
        body,
        mesh=fine,
        in_specs=(P(groups), P(segment, groups), P(groups, segment)),
        out_specs=(P(groups, None), P(segment, groups)),
        check_vma=False,
    )
```

time: 368 us -> 145 us (0.39)
  local copies, waits for them, and re-layouts: 76.5 us -> 5.02 us
  waiting for transfers between devices: 102 us -> 36.8 us
  blocking collectives: 93.4 us -> 32.9 us
  other arithmetic: 23.6 us -> 4.19 us
  between operations: 14.3 us -> 0.94 us
  matrix products: 0 us -> 5.85 us
    all_gather x2, blocking collectives: 93.4 us -> 32.9 us  [the longest x1 20.5 us: body(): halves = lax.all_gather(out_grad, ('y', 'core'), axis=1, tiled=True)]
    reduce_scatter x1 -> x0, waiting for transfers between devices: 52.1 us -> none  [sum_in_two_steps(): own = lax.psum_scatter(padded, axis, scatter_dimension=0, tiled=True)]
    all_to_all x3, waiting for transfers between devices: 49.5 us -> 11 us  [the longest x1 11 us: body(): lax.all_to_all(jnp.broadcast_to(token_ids[None], (32, tokens)), GROUPS, 0...]
    unnamed x19 -> x2, local copies, waits for them, and re-layouts: 36 us -> 0.01 us
    ppermute x0 -> x4, waiting for transfers between devices: none -> 25.8 us  [the longest x3 25.8 us: move(): return lax.ppermute(values, NAMES, pairs)]
    all_to_all x3, starting transfers between devices: 57.4 us -> 32.3 us  [the longest x1 15.9 us: body(): lax.all_to_all(jnp.broadcast_to(token_ids[None], (32, tokens)), GROUPS, 0...]
    ppermute x0 -> x4, starting transfers between devices: none -> 25 us  [the longest x3 19.7 us: move(): return lax.ppermute(values, NAMES, pairs)]
    scatter x4 -> x0, local copies, waits for them, and re-layouts: 13 us -> none  [the longest x1 6.48 us: body(): jnp.zeros((PACK, capacity), jnp.bool_).at[slot_place, my_rank]]
  transfers between devices with their start and end apart: 4 -> 7, of which waited for: 3 -> 4; matrix products, arithmetic and copies ran while one was open for 12% -> 5% of each run, Pallas kernels for 0% -> 0%
where the time goes in v1:
time: 145 us; the launch traced here: 143 us
  starting transfers between devices  57.3 us (40%)
  waiting for transfers between devices  36.8 us (25%)
  blocking collectives  32.9 us (23%)
  matrix products  5.85 us (4%)
  local copies, waits for them, and re-layouts  5.02 us (3%)
  other arithmetic  4.19 us (3%)
    ppermute x3, waiting for transfers between devices, move(): return lax.ppermute(values, NAMES, pairs)  25.8 us
    all_gather x1, blocking collectives, body(): halves = lax.all_gather(out_grad, ('y', 'core'), axis=1, tiled=True)  20.5 us
    ppermute x3, starting transfers between devices, move(): return lax.ppermute(values, NAMES, pairs)  19.7 us
    all_to_all x1, starting transfers between devices, body(): lax.all_to_all(jnp.broadcast_to(token_ids[None], (32, tokens)), GROUPS, 0...  15.9 us
    all_gather x1, blocking collectives, body(): whole = lax.all_gather(quarter, 'y')  12.4 us
    all_to_all x1, waiting for transfers between devices, body(): lax.all_to_all(jnp.broadcast_to(token_ids[None], (32, tokens)), GROUPS, 0...  11 us
    all_to_all x1, starting transfers between devices, body(): lax.all_to_all(packed.reshape(32, SLOTS, width), PLANE, 0, 0, tiled=True)  8.99 us
    all_to_all x1, starting transfers between devices, body(): lax.all_to_all(fetched.reshape(32, SLOTS, width), PLANE, 0, 0, tiled=True)  7.41 us
  transfers between devices with their start and end apart: 7, of which 4 were waited for; matrix products, arithmetic and copies ran while one was open for 5% of the time, Pallas kernels for 0%

profile of v1, /device:TPU:1, one launch (start us, length us, event | category | flops | bytes accessed | tf_op | source)
XLA Modules:
  0.0 143.0 jit_solution(15806224102012464601)
XLA Ops:
  0.6 1.4 broadcast_in_dim.37
  2.1 15.9 %all-to-all-start = ((s32[32,1,128]{2,1,0:T(1,128)}), s32[32,1,128]{2,1,0:T(1,128)S(1)}, u32[]{:S(2)}, u32[]{:S(2)}) async-start(s32[32,1,128]{2,1,0:T(1,128)} %broadcast_in_dim.37), calls=%async_computation | async-start | bytes 32768 | tf_op jit(solution)/shard_map/all_to_all | solution.py:76
  18.1 0.1 fusion.25
  18.1 0.1 compare_and_fusion
  18.2 11.0 %all-to-all-done = s32[32,1,128]{2,1,0:T(1,128)S(1)} async-done(((s32[32,1,128]{2,1,0:T(1,128)}), s32[32,1,128]{2,1,0:T(1,128)S(1)}, u32[]{:S(2)}, u32[]{:S(2)}) %all-to-all-start) | async-done | bytes 16416 | tf_op jit(solution)/shard_map/all_to_all | solution.py:76
  29.3 0.6 gather_fusion
  29.9 0.1 fusion.9
  30.0 0.1 fusion.11
  30.1 0.1 convolution_convert_fusion.3
  30.2 1.2 select_reduce_fusion
  31.4 0.1 reshape.480
  31.5 2.1 %gather_fusion.1 = bf16[512,896]{1,0:T(8,128)(2,1)S(1)} fusion(bf16[1188,896]{1,0:T(8,128)(2,1)S(1)} %copy-done, s32[1024]{0:T(1024)S(1)} %pad_clamp_fusion), kind=kCustom, calls=%fused_computation.1 | custom fusion | bytes 1837056 | tf_op jit(solution)/shard_map/jit(_take)/gather | solution.py:94
  33.6 1.1 broadcast_select_fusion
  34.7 7.4 %all-to-all-start.1 = ((bf16[32,16,896]{2,1,0:T(8,128)(2,1)}), bf16[32,16,896]{2,1,0:T(8,128)(2,1)S(1)}, u32[]{:S(2)}, u32[]{:S(2)}) async-start(bf16[32,16,896]{2,1,0:T(8,128)(2,1)} %broadcast_select_fusion), calls=%async_computation.1 | async-start | bytes 1835008 | tf_op jit(solution)/shard_map/all_to_all | solution.py:95
  42.1 20.5 %all_gather.11 = bf16[128,1792]{0,1:T(8,128)(2,1)S(1)} all-gather(bf16[128,224]{0,1:T(8,128)(2,1)} %param.5), channel_id=1, replica_groups=mesh['z_hi'=2,'y'=4,'core'=2,'x'=4,'z_lo'=8] {'y','core'}, dimensions={1}, use_global_device_ids=true | all-gather | bytes 516096 | tf_op jit(solution)/shard_map/all_gather | solution.py:119
  62.6 0.7 constant_dynamic-slice_fusion
  63.3 7.9 %collective-permute-start.3 = (bf16[128,896]{0,1:T(8,128)(2,1)}, bf16[128,896]{0,1:T(8,128)(2,1)S(1)}, u32[]{:S(2)}, u32[]{:S(2)}) collective-permute-start(bf16[128,896]{0,1:T(8,128)(2,1)} %constant_dynamic-slice_fusion), channel_id=1, source_target_pairs={{0,0},{1,1},{2,4},{3,5},{4,256},{5,257},{6,260},{7,261},{8,8},{9,9... | collective-permute-start | bytes 688136 | tf_op jit(solution)/shard_map/ppermute | solution.py:31
  71.3 0.2 convert_reduce_fusion
  71.5 9.0 %collective-permute-done.3 = bf16[128,896]{0,1:T(8,128)(2,1)S(1)} collective-permute-done((bf16[128,896]{0,1:T(8,128)(2,1)}, bf16[128,896]{0,1:T(8,128)(2,1)S(1)}, u32[]{:S(2)}, u32[]{:S(2)}) %collective-permute-start.3) | collective-permute-done | bytes 229408 | tf_op jit(solution)/shard_map/ppermute | solution.py:31
  80.5 1.4 convolution_convert_fusion.1
  82.0 9.0 %all-to-all-start.2 = ((bf16[32,16,896]{2,1,0:T(8,128)(2,1)}), bf16[32,16,896]{2,1,0:T(8,128)(2,1)}, u32[]{:S(2)}, u32[]{:S(2)}) async-start(bf16[32,16,896]{2,1,0:T(8,128)(2,1)} %bitcast.54), calls=%async_computation.2 | async-start | bytes 1835008 | tf_op jit(solution)/shard_map/all_to_all | solution.py:128
  91.0 0.2 convert_reduce_fusion.1
  91.2 0.4 convolution_convert_fusion.2
  91.5 6.3 %collective-permute-start.1 = (bf16[128,896]{1,0:T(8,128)(2,1)S(1)}, bf16[128,896]{1,0:T(8,128)(2,1)S(1)}, u32[]{:S(2)}, u32[]{:S(2)}) collective-permute-start(bf16[128,896]{1,0:T(8,128)(2,1)S(1)} %convolution_convert_fusion.2), channel_id=1, source_target_pairs={{0,256},{1,257},{2,258},{3,259},{4,260},{5,261},{6,262},{7,263},{8... | collective-permute-start | bytes 688136 | tf_op jit(solution)/shard_map/ppermute | solution.py:31
  97.9 5.4 %collective-permute-start = (bf16[128,896]{1,0:T(8,128)(2,1)S(1)}, bf16[128,896]{1,0:T(8,128)(2,1)S(1)}, u32[]{:S(2)}, u32[]{:S(2)}) collective-permute-start(bf16[128,896]{1,0:T(8,128)(2,1)S(1)} %convolution_convert_fusion.2), channel_id=1, source_target_pairs={{0,0},{1,1},{2,2},{3,3},{4,4},{5,5},{6,6},{7,7},{8,8},{9,9},{10,10... | collective-permute-start | bytes 688136 | tf_op jit(solution)/shard_map/ppermute | solution.py:31
  103.3 0.1 eq.165
  103.4 11.2 %collective-permute-done.1 = bf16[128,896]{1,0:T(8,128)(2,1)S(1)} collective-permute-done((bf16[128,896]{1,0:T(8,128)(2,1)S(1)}, bf16[128,896]{1,0:T(8,128)(2,1)S(1)}, u32[]{:S(2)}, u32[]{:S(2)}) %collective-permute-start.1) | collective-permute-done | bytes 229408 | tf_op jit(solution)/shard_map/ppermute | solution.py:31
  114.6 5.5 %collective-permute-done = bf16[128,896]{1,0:T(8,128)(2,1)S(1)} collective-permute-done((bf16[128,896]{1,0:T(8,128)(2,1)S(1)}, bf16[128,896]{1,0:T(8,128)(2,1)S(1)}, u32[]{:S(2)}, u32[]{:S(2)}) %collective-permute-start) | collective-permute-done | bytes 229408 | tf_op jit(solution)/shard_map/ppermute | solution.py:31
  120.2 5.3 %collective-permute-start.2 = (bf16[128,896]{1,0:T(8,128)(2,1)S(1)}, bf16[128,896]{1,0:T(8,128)(2,1)S(1)}, u32[]{:S(2)}, u32[]{:S(2)}) collective-permute-start(bf16[128,896]{1,0:T(8,128)(2,1)S(1)} %add.524), channel_id=1, source_target_pairs={{0,32},{32,0},{1,33},{33,1},{2,34},{34,2},{3,35},{35,3},{4,36},{36... | collective-permute-start | bytes 688136 | tf_op jit(solution)/shard_map/ppermute | solution.py:109
  125.5 3.9 %convolution_convert_fusion = bf16[1188,896]{1,0:T(8,128)(2,1)} fusion(bf16[512,896]{1,0:T(8,128)(2,1)} %bitcast.19, s32[512]{0:T(512)S(1)} %eq.165), kind=kOutput, calls=%fused_computation.2 | convolution fusion | flops 1091667456 | bytes 3048448 | tf_op jit(solution)/shard_map/dot_general | solution.py:131
  129.5 12.4 %all-gather = bf16[512,896]{1,0:T(8,128)(2,1)S(1)} all-gather(bf16[128,896]{1,0:T(8,128)(2,1)S(1)} %add.525), channel_id=2, replica_groups=mesh['z_hi'=2,'y'=4,'core'=2,'x'=4,'z_lo'=8] {'y'}, dimensions={0}, use_global_device_ids=true | all-gather | bytes 1146880 | tf_op jit(solution)/shard_map/all_gather | solution.py:110
  142.0 1.0 pad_maximum_fusion
  (19 shorter events, 0.3 us)
Async XLA Ops:
  0.6 30.9 %copy-start = (bf16[1188,896]{1,0:T(8,128)(2,1)S(1)}, bf16[1188,896]{1,0:T(8,128)(2,1)}, u32[]{:S(2)}) copy-start(bf16[1188,896]{1,0:T(8,128)(2,1)} %param.4) | copy-start | bytes 6386692
  2.1 27.2 %all-to-all-start = ((s32[32,1,128]{2,1,0:T(1,128)}), s32[32,1,128]{2,1,0:T(1,128)S(1)}, u32[]{:S(2)}, u32[]{:S(2)}) async-start(s32[32,1,128]{2,1,0:T(1,128)} %broadcast_in_dim.37), calls=%async_computation | async-start | bytes 32768 | tf_op jit(solution)/shard_map/all_to_all | solution.py:76
  34.7 47.3 %all-to-all-start.1 = ((bf16[32,16,896]{2,1,0:T(8,128)(2,1)}), bf16[32,16,896]{2,1,0:T(8,128)(2,1)S(1)}, u32[]{:S(2)}, u32[]{:S(2)}) async-start(bf16[32,16,896]{2,1,0:T(8,128)(2,1)} %broadcast_select_fusion), calls=%async_computation.1 | async-start | bytes 1835008 | tf_op jit(solution)/shard_map/all_to_all | solution.py:95
  63.3 17.2 %collective-permute-start.3 = (bf16[128,896]{0,1:T(8,128)(2,1)}, bf16[128,896]{0,1:T(8,128)(2,1)S(1)}, u32[]{:S(2)}, u32[]{:S(2)}) collective-permute-start(bf16[128,896]{0,1:T(8,128)(2,1)} %constant_dynamic-slice_fusion), channel_id=1, source_target_pairs={{0,0},{1,1},{2,4},{3,5},{4,256},{5,257},{6,260},{7,261},{8,8},{9,9... | collective-permute-start | bytes 688136 | tf_op jit(solution)/shard_map/ppermute | solution.py:31
  82.0 43.6 %all-to-all-start.2 = ((bf16[32,16,896]{2,1,0:T(8,128)(2,1)}), bf16[32,16,896]{2,1,0:T(8,128)(2,1)}, u32[]{:S(2)}, u32[]{:S(2)}) async-start(bf16[32,16,896]{2,1,0:T(8,128)(2,1)} %bitcast.54), calls=%async_computation.2 | async-start | bytes 1835008 | tf_op jit(solution)/shard_map/all_to_all | solution.py:128
  91.5 23.1 %collective-permute-start.1 = (bf16[128,896]{1,0:T(8,128)(2,1)S(1)}, bf16[128,896]{1,0:T(8,128)(2,1)S(1)}, u32[]{:S(2)}, u32[]{:S(2)}) collective-permute-start(bf16[128,896]{1,0:T(8,128)(2,1)S(1)} %convolution_convert_fusion.2), channel_id=1, source_target_pairs={{0,256},{1,257},{2,258},{3,259},{4,260},{5,261},{6,262},{7,263},{8... | collective-permute-start | bytes 688136 | tf_op jit(solution)/shard_map/ppermute | solution.py:31
  97.9 22.3 %collective-permute-start = (bf16[128,896]{1,0:T(8,128)(2,1)S(1)}, bf16[128,896]{1,0:T(8,128)(2,1)S(1)}, u32[]{:S(2)}, u32[]{:S(2)}) collective-permute-start(bf16[128,896]{1,0:T(8,128)(2,1)S(1)} %convolution_convert_fusion.2), channel_id=1, source_target_pairs={{0,0},{1,1},{2,2},{3,3},{4,4},{5,5},{6,6},{7,7},{8,8},{9,9},{10,10... | collective-permute-start | bytes 688136 | tf_op jit(solution)/shard_map/ppermute | solution.py:31
  120.2 9.3 %collective-permute-start.2 = (bf16[128,896]{1,0:T(8,128)(2,1)S(1)}, bf16[128,896]{1,0:T(8,128)(2,1)S(1)}, u32[]{:S(2)}, u32[]{:S(2)}) collective-permute-start(bf16[128,896]{1,0:T(8,128)(2,1)S(1)} %add.524), channel_id=1, source_target_pairs={{0,32},{32,0},{1,33},{33,1},{2,34},{34,2},{3,35},{35,3},{4,36},{36... | collective-permute-start | bytes 688136 | tf_op jit(solution)/shard_map/ppermute | solution.py:109

commit v2 on v1

--- a/solution.py
+++ b/solution.py
@@ -5,7 +5,7 @@
 from jax import lax
 from jax.sharding import Mesh, PartitionSpec as P
 
-D = 3584
+
 PACK = 8
 SLOTS = 16
 NAMES = ("z_hi", "y", "core", "x", "z_lo")
@@ -13,7 +13,6 @@
 PLANE = ("y", "core", "x")
 GROUPS = ("x", "z_lo")
 QUARTERS = 4
-WIDTH = D // QUARTERS
 BF16 = jnp.bfloat16
 
 
@@ -29,10 +28,6 @@
         for place in itertools.product(*(range(size) for size in SIZES))
     ]
     return lax.ppermute(values, NAMES, pairs)
-
-
-def lookup_code(z_hi, z_lo):
-    return z_lo
 
 
 def grad_code(z_hi, z_lo):
@@ -76,11 +71,16 @@
     every_id = lax.all_to_all(
         jnp.broadcast_to(token_ids[None], (32, tokens)), GROUPS, 0, 0, tiled=True
     )
+    halves = lax.all_gather(out_grad, ("y", "core"), axis=1, tiled=True)
+    every_id, halves = lax.optimization_barrier((every_id, halves))
+    which = (place ^ z_lo) % 2
+    piece = lax.dynamic_slice(halves, (0, which * width), (tokens, width))
+    piece = move(piece, grad_target)
 
-    code_f = lookup_code(z_hi, z_lo)
+    code_f = z_lo
     code_b = grad_code(z_hi, z_lo)
     orders = jnp.concatenate([groups_of_plane(code_f), groups_of_plane(code_b)])
-    ids = jnp.take(every_id, orders, axis=0)
+    ids = jnp.take(every_id, orders, axis=0, mode="clip")
     local = ids - segment * section
     owned = (local >= 0) & (local < section) & (local % PACK == residue)
     line = local // PACK
@@ -91,7 +91,7 @@
     hit = owned[:, None, :] & (rank[:, None, :] == slots[None, :, None])
     row_of = jnp.sum(jnp.where(hit, line[:, None, :] + 1, 0), axis=2) - 1
 
-    fetched = jnp.take(table, jnp.maximum(row_of[:32], 0).reshape(-1), axis=0)
+    fetched = jnp.take(table, jnp.maximum(row_of[:32], 0).reshape(-1), axis=0, mode="clip")
     arrived = lax.all_to_all(fetched.reshape(32, SLOTS, width), PLANE, 0, 0, tiled=True)
     ids_f = lax.dynamic_index_in_dim(every_id, x * 8 + (place ^ code_f), 0, keepdims=False)
     pick_f = pick_matrix(ids_f, section, z_hi, parity)
@@ -116,10 +116,6 @@
         axis=1,
     )
 
-    halves = lax.all_gather(out_grad, ("y", "core"), axis=1, tiled=True)
-    which = (place ^ z_lo) % 2
-    piece = lax.dynamic_slice(halves, (0, which * width), (tokens, width))
-    piece = move(piece, grad_target)
     ids_b = lax.dynamic_index_in_dim(every_id, x * 8 + (place ^ code_b), 0, keepdims=False)
     pick_b = pick_matrix(ids_b, section, z_hi, parity)
     packed = lax.dot_general(
@@ -137,6 +133,7 @@
 def solution(mesh):
     fine = Mesh(mesh.devices.reshape(SIZES), NAMES)
     segment, groups = ("z_hi", "y", "core"), ("x", "z_lo")
+
     return jax.shard_map(
         body,
         mesh=fine,

time: 145 us -> 128 us (0.88)
  the two profiles are of different devices: /device:TPU:1 before, /device:TPU:2 now
where the time goes in v2:
time: 128 us
  starting transfers between devices  52.3 us (41%)
  waiting for transfers between devices  31.5 us (25%)
  blocking collectives  28.8 us (22%)
  matrix products  5.85 us (5%)
  local copies, waits for them, and re-layouts  5.02 us (4%)
  other arithmetic  3.43 us (3%)
    ppermute x3, waiting for transfers between devices, move(): return lax.ppermute(values, NAMES, pairs)  20.5 us
    all_to_all x1, starting transfers between devices, body(): lax.all_to_all(jnp.broadcast_to(token_ids[None], (32, tokens)), GROUPS, 0...  15.7 us
    all_gather x1, blocking collectives, body(): whole = lax.all_gather(quarter, 'y')  15 us
    all_to_all x1, starting transfers between devices, body(): lax.all_to_all(fetched.reshape(32, SLOTS, width), PLANE, 0, 0, tiled=True)  14.4 us
    all_gather x1, blocking collectives, body(): halves = lax.all_gather(out_grad, ('y', 'core'), axis=1, tiled=True)  13.8 us
    ppermute x3, starting transfers between devices, move(): return lax.ppermute(values, NAMES, pairs)  11.1 us
    all_to_all x1, waiting for transfers between devices, body(): lax.all_to_all(fetched.reshape(32, SLOTS, width), PLANE, 0, 0, tiled=True)  11 us
    all_to_all x1, starting transfers between devices, body(): lax.all_to_all(packed.reshape(32, SLOTS, width), PLANE, 0, 0, tiled=True)  6.91 us
  transfers between devices with their start and end apart: 7, of which 2 were waited for; matrix products, arithmetic and copies ran while one was open for 8% of the time, Pallas kernels for 0%

profile of v2, /device:TPU:2, one launch (start us, length us, event | category | flops | bytes accessed | tf_op | source)
XLA Modules:
  0.0 127.8 jit_solution(1511386621162301404)
XLA Ops:
  0.6 0.0 copy-start
  0.6 1.4 %broadcast_in_dim.24 = s32[32,1,128]{2,1,0:T(1,128)} broadcast(s32[128]{0:T(128)} %param.3), dimensions={2} | broadcast | bytes 16896 | tf_op jit(solution)/shard_map/broadcast_in_dim | solution.py:72
  2.1 15.7 %all-to-all-start = ((s32[32,1,128]{2,1,0:T(1,128)}), s32[32,1,128]{2,1,0:T(1,128)S(1)}, u32[]{:S(2)}, u32[]{:S(2)}) async-start(s32[32,1,128]{2,1,0:T(1,128)} %broadcast_in_dim.24), calls=%async_computation | async-start | bytes 32768 | tf_op jit(solution)/shard_map/all_to_all | solution.py:71
  17.8 13.8 %all_gather.9 = bf16[128,1792]{0,1:T(8,128)(2,1)S(1)} all-gather(bf16[128,224]{0,1:T(8,128)(2,1)} %param.5), channel_id=1, replica_groups=mesh['z_hi'=2,'y'=4,'core'=2,'x'=4,'z_lo'=8] {'y','core'}, dimensions={1}, use_global_device_ids=true | all-gather | bytes 516096 | tf_op jit(solution)/shard_map/all_gather | solution.py:74
  31.6 0.1 pad_add_fusion
  31.7 0.0 all-to-all-done
  31.7 0.6 gather_fusion
  32.4 0.1 convolution_convert_fusion.3
  32.5 1.2 select_reduce_fusion
  33.7 0.1 reshape.300
  33.8 0.7 collective-permute-start.3
  34.5 2.7 %gather_fusion.1 = bf16[512,896]{1,0:T(8,128)(2,1)} fusion(bf16[1188,896]{1,0:T(8,128)(2,1)S(1)} %copy-done, s32[1024]{0:T(1024)S(1)} %pad_clamp_fusion), kind=kCustom, calls=%fused_computation.1 | custom fusion | bytes 1837056 | tf_op jit(solution)/shard_map/jit(_take)/gather | solution.py:94
  37.3 14.4 %all-to-all-start.1 = ((bf16[32,16,896]{2,1,0:T(8,128)(2,1)}), bf16[32,16,896]{2,1,0:T(8,128)(2,1)S(1)}, u32[]{:S(2)}, u32[]{:S(2)}) async-start(bf16[32,16,896]{2,1,0:T(8,128)(2,1)} %bitcast.5), calls=%async_computation.1 | async-start | bytes 1835008 | tf_op jit(solution)/shard_map/all_to_all | solution.py:95
  51.7 0.6 multiply_add_fusion
  52.2 0.2 convert_reduce_fusion
  52.5 1.4 %convolution_convert_fusion.1 = bf16[512,896]{1,0:T(8,128)(2,1)} fusion(bf16[128,896]{0,1:T(8,128)(2,1)S(1)} %collective-permute-done.3, s32[128]{0:T(128)S(1)} %and_select_fusion.5), kind=kOutput, calls=%fused_computation.4 | convolution fusion | flops 118030336 | bytes 1147392 | tf_op jit(solution)/shard_map/dot_general | solution.py:121
  53.9 11.0 %all-to-all-done.1 = bf16[32,16,896]{2,1,0:T(8,128)(2,1)S(1)} async-done(((bf16[32,16,896]{2,1,0:T(8,128)(2,1)}), bf16[32,16,896]{2,1,0:T(8,128)(2,1)S(1)}, u32[]{:S(2)}, u32[]{:S(2)}) %all-to-all-start.1) | async-done | bytes 917536 | tf_op jit(solution)/shard_map/all_to_all | solution.py:95
  64.9 6.9 %all-to-all-start.2 = ((bf16[32,16,896]{2,1,0:T(8,128)(2,1)}), bf16[32,16,896]{2,1,0:T(8,128)(2,1)}, u32[]{:S(2)}, u32[]{:S(2)}) async-start(bf16[32,16,896]{2,1,0:T(8,128)(2,1)} %bitcast.16), calls=%async_computation.2 | async-start | bytes 1835008 | tf_op jit(solution)/shard_map/all_to_all | solution.py:124
  71.9 0.2 convert_reduce_fusion.1
  72.1 0.4 convolution_convert_fusion.2
  72.5 9.7 %collective-permute-start.1 = (bf16[128,896]{1,0:T(8,128)(2,1)S(1)}, bf16[128,896]{1,0:T(8,128)(2,1)S(1)}, u32[]{:S(2)}, u32[]{:S(2)}) collective-permute-start(bf16[128,896]{1,0:T(8,128)(2,1)S(1)} %convolution_convert_fusion.2), channel_id=1, source_target_pairs={{0,256},{1,257},{2,258},{3,259},{4,260},{5,261},{6,262},{7,263},{8... | collective-permute-start | bytes 688136 | tf_op jit(solution)/shard_map/ppermute | solution.py:30
  82.2 0.7 collective-permute-start
  82.9 0.1 eq.170
  83.0 20.5 %collective-permute-done.1 = bf16[128,896]{1,0:T(8,128)(2,1)S(1)} collective-permute-done((bf16[128,896]{1,0:T(8,128)(2,1)S(1)}, bf16[128,896]{1,0:T(8,128)(2,1)S(1)}, u32[]{:S(2)}, u32[]{:S(2)}) %collective-permute-start.1) | collective-permute-done | bytes 229408 | tf_op jit(solution)/shard_map/ppermute | solution.py:30
  103.4 0.0 collective-permute-done
  103.4 0.1 add.326
  103.5 4.2 %collective-permute-start.2 = (bf16[128,896]{1,0:T(8,128)(2,1)S(1)}, bf16[128,896]{1,0:T(8,128)(2,1)S(1)}, u32[]{:S(2)}, u32[]{:S(2)}) collective-permute-start(bf16[128,896]{1,0:T(8,128)(2,1)S(1)} %add.326), channel_id=1, source_target_pairs={{0,32},{32,0},{1,33},{33,1},{2,34},{34,2},{3,35},{35,3},{4,36},{36... | collective-permute-start | bytes 688136 | tf_op jit(solution)/shard_map/ppermute | solution.py:109
  107.7 3.9 %convolution_convert_fusion = bf16[1188,896]{1,0:T(8,128)(2,1)} fusion(bf16[512,896]{1,0:T(8,128)(2,1)} %bitcast.17, s32[512]{0:T(512)S(1)} %eq.170), kind=kOutput, calls=%fused_computation.2 | convolution fusion | flops 1091667456 | bytes 3048448 | tf_op jit(solution)/shard_map/dot_general | solution.py:127
  111.7 0.1 add.327
  111.8 15.0 %all-gather = bf16[512,896]{1,0:T(8,128)(2,1)S(1)} all-gather(bf16[128,896]{1,0:T(8,128)(2,1)S(1)} %add.327), channel_id=2, replica_groups=mesh['z_hi'=2,'y'=4,'core'=2,'x'=4,'z_lo'=8] {'y'}, dimensions={0}, use_global_device_ids=true | all-gather | bytes 1146880 | tf_op jit(solution)/shard_map/all_gather | solution.py:110
  126.7 0.1 dynamic-slice_bitcast_fusion.3
  126.8 1.0 pad_maximum_fusion
  (20 shorter events, 0.2 us)
Async XLA Ops:
  0.6 33.9 %copy-start = (bf16[1188,896]{1,0:T(8,128)(2,1)S(1)}, bf16[1188,896]{1,0:T(8,128)(2,1)}, u32[]{:S(2)}) copy-start(bf16[1188,896]{1,0:T(8,128)(2,1)} %param.4) | copy-start | bytes 6386692
  2.1 29.6 %all-to-all-start = ((s32[32,1,128]{2,1,0:T(1,128)}), s32[32,1,128]{2,1,0:T(1,128)S(1)}, u32[]{:S(2)}, u32[]{:S(2)}) async-start(s32[32,1,128]{2,1,0:T(1,128)} %broadcast_in_dim.24), calls=%async_computation | async-start | bytes 32768 | tf_op jit(solution)/shard_map/all_to_all | solution.py:71
  33.8 18.6 %collective-permute-start.3 = (bf16[128,896]{0,1:T(8,128)(2,1)S(1)}, bf16[128,896]{0,1:T(8,128)(2,1)S(1)}, u32[]{:S(2)}, u32[]{:S(2)}) collective-permute-start(bf16[128,896]{0,1:T(8,128)(2,1)S(1)} %constant_dynamic-slice_fusion), channel_id=1, source_target_pairs={{0,0},{1,1},{2,4},{3,5},{4,256},{5,257},{6,260},{7,261},{8,8},{9,9... | collective-permute-start | bytes 688136 | tf_op jit(solution)/shard_map/ppermute | solution.py:30
  37.3 27.7 %all-to-all-start.1 = ((bf16[32,16,896]{2,1,0:T(8,128)(2,1)}), bf16[32,16,896]{2,1,0:T(8,128)(2,1)S(1)}, u32[]{:S(2)}, u32[]{:S(2)}) async-start(bf16[32,16,896]{2,1,0:T(8,128)(2,1)} %bitcast.5), calls=%async_computation.1 | async-start | bytes 1835008 | tf_op jit(solution)/shard_map/all_to_all | solution.py:95
  52.2 19.6 %copy-start.1 = (s32[1,128]{1,0:T(1,128)S(1)}, s32[1,128]{1,0:T(1,128)}, u32[]{:S(2)}) copy-start(s32[1,128]{1,0:T(1,128)} %get-tuple-element.23) | copy-start | bytes 1540
  52.2 19.7 %copy-start.2 = (s32[128]{0:T(128)S(1)}, s32[128]{0:T(128)}, u32[]{:S(2)}) copy-start(s32[128]{0:T(128)} %get-tuple-element.20) | copy-start | bytes 1540
  64.9 42.8 %all-to-all-start.2 = ((bf16[32,16,896]{2,1,0:T(8,128)(2,1)}), bf16[32,16,896]{2,1,0:T(8,128)(2,1)}, u32[]{:S(2)}, u32[]{:S(2)}) async-start(bf16[32,16,896]{2,1,0:T(8,128)(2,1)} %bitcast.16), calls=%async_computation.2 | async-start | bytes 1835008 | tf_op jit(solution)/shard_map/all_to_all | solution.py:124
  72.5 31.0 %collective-permute-start.1 = (bf16[128,896]{1,0:T(8,128)(2,1)S(1)}, bf16[128,896]{1,0:T(8,128)(2,1)S(1)}, u32[]{:S(2)}, u32[]{:S(2)}) collective-permute-start(bf16[128,896]{1,0:T(8,128)(2,1)S(1)} %convolution_convert_fusion.2), channel_id=1, source_target_pairs={{0,256},{1,257},{2,258},{3,259},{4,260},{5,261},{6,262},{7,263},{8... | collective-permute-start | bytes 688136 | tf_op jit(solution)/shard_map/ppermute | solution.py:30
  82.2 21.3 %collective-permute-start = (bf16[128,896]{1,0:T(8,128)(2,1)S(1)}, bf16[128,896]{1,0:T(8,128)(2,1)S(1)}, u32[]{:S(2)}, u32[]{:S(2)}) collective-permute-start(bf16[128,896]{1,0:T(8,128)(2,1)S(1)} %convolution_convert_fusion.2), channel_id=1, source_target_pairs={{0,0},{1,1},{2,2},{3,3},{4,4},{5,5},{6,6},{7,7},{8,8},{9,9},{10,10... | collective-permute-start | bytes 688136 | tf_op jit(solution)/shard_map/ppermute | solution.py:30
  103.5 8.2 %collective-permute-start.2 = (bf16[128,896]{1,0:T(8,128)(2,1)S(1)}, bf16[128,896]{1,0:T(8,128)(2,1)S(1)}, u32[]{:S(2)}, u32[]{:S(2)}) collective-permute-start(bf16[128,896]{1,0:T(8,128)(2,1)S(1)} %add.326), channel_id=1, source_target_pairs={{0,32},{32,0},{1,33},{33,1},{2,34},{34,2},{3,35},{35,3},{4,36},{36... | collective-permute-start | bytes 688136 | tf_op jit(solution)/shard_map/ppermute | solution.py:109

commit v3 on v2

--- a/solution.py
+++ b/solution.py
@@ -1,3 +1,4 @@
+import functools
 import itertools
 
 import jax
@@ -34,9 +35,16 @@
     return z_hi * 4 + (z_lo // 4) * 2 + z_lo % 2
 
 
-def grad_target(z_hi, y, core, x, z_lo):
-    code = (core * 4 + y) ^ z_lo
-    return (code // 4, y, core, x, ((code // 2) % 2) * 4 + 2 * z_hi + code % 2)
+def grad_target(k, z_hi, y, core, x, z_lo):
+    high, low = y // 2, y % 2
+    parity = k ^ low ^ ((z_lo // 2) % 2)
+    return (
+        core ^ (z_lo // 4),
+        2 * (k ^ low) + ((z_lo % 2) ^ high),
+        core,
+        x,
+        parity * 4 + 2 * z_hi + high,
+    )
 
 
 def groups_of_plane(code):
@@ -71,11 +79,14 @@
     every_id = lax.all_to_all(
         jnp.broadcast_to(token_ids[None], (32, tokens)), GROUPS, 0, 0, tiled=True
     )
-    halves = lax.all_gather(out_grad, ("y", "core"), axis=1, tiled=True)
-    every_id, halves = lax.optimization_barrier((every_id, halves))
-    which = (place ^ z_lo) % 2
-    piece = lax.dynamic_slice(halves, (0, which * width), (tokens, width))
-    piece = move(piece, grad_target)
+    own = out_grad.T
+    other = move(own, lambda a, b, c, d, e: (a, b, 1 - c, d, e))
+    half = jnp.concatenate(
+        [jnp.where(core == 0, own, other), jnp.where(core == 0, other, own)]
+    )
+    early = move(half, functools.partial(grad_target, 0))
+    late = move(half, functools.partial(grad_target, 1))
+    sent = (early, late)
 
     code_f = z_lo
     code_b = grad_code(z_hi, z_lo)
@@ -118,8 +129,12 @@
 
     ids_b = lax.dynamic_index_in_dim(every_id, x * 8 + (place ^ code_b), 0, keepdims=False)
     pick_b = pick_matrix(ids_b, section, z_hi, parity)
+    swapped = y // 2 == 1
+    piece = jnp.concatenate(
+        [jnp.where(swapped, sent[1], sent[0]), jnp.where(swapped, sent[0], sent[1])]
+    )
     packed = lax.dot_general(
-        pick_b, piece, (((0,), (0,)), ((), ())), preferred_element_type=jnp.float32
+        pick_b, piece, (((0,), (1,)), ((), ())), preferred_element_type=jnp.float32
     ).astype(BF16)
     returned = lax.all_to_all(packed.reshape(32, SLOTS, width), PLANE, 0, 0, tiled=True)
     target = row_of[32:].reshape(-1)

time: 128 us -> 127 us (level)
  the two profiles are of different devices: /device:TPU:2 before, /device:TPU:1 now
where the time goes in v3:
time: 127 us; the launch traced here: 125 us
  starting transfers between devices  62.2 us (49%)
  waiting for transfers between devices  34.6 us (27%)
  blocking collectives  12.7 us (10%)
  matrix products  5.85 us (5%)
  local copies, waits for them, and re-layouts  4.99 us (4%)
  other arithmetic  3.71 us (3%)
    ppermute x5, starting transfers between devices, move(): return lax.ppermute(values, NAMES, pairs)  24.4 us
    ppermute x5, waiting for transfers between devices, move(): return lax.ppermute(values, NAMES, pairs)  21.4 us
    all_to_all x1, starting transfers between devices, body(): lax.all_to_all(jnp.broadcast_to(token_ids[None], (32, tokens)), GROUPS, 0...  15.9 us
    all_to_all x1, waiting for transfers between devices, body(): lax.all_to_all(fetched.reshape(32, SLOTS, width), PLANE, 0, 0, tiled=True)  13.2 us
    all_gather x1, blocking collectives, body(): whole = lax.all_gather(quarter, 'y')  12.7 us
    all_to_all x1, starting transfers between devices, body(): lax.all_to_all(fetched.reshape(32, SLOTS, width), PLANE, 0, 0, tiled=True)  10.8 us
    ppermute x1, starting transfers between devices, body(): quarter = both + lax.ppermute(both, 'core', [(0, 1), (1, 0)])  5.72 us
    all_to_all x1, starting transfers between devices, body(): lax.all_to_all(packed.reshape(32, SLOTS, width), PLANE, 0, 0, tiled=True)  5.33 us
  transfers between devices with their start and end apart: 9, of which 4 were waited for; matrix products, arithmetic and copies ran while one was open for 10% of the time, Pallas kernels for 0%

profile of v3, /device:TPU:1, one launch (start us, length us, event | category | flops | bytes accessed | tf_op | source)
XLA Modules:
  0.0 125.0 jit_solution(6736067090547845354)
XLA Ops:
  0.6 1.4 %broadcast_in_dim.24 = s32[32,1,128]{2,1,0:T(1,128)} broadcast(s32[128]{0:T(128)} %param.3), dimensions={2} | broadcast | bytes 16896 | tf_op jit(solution)/shard_map/broadcast_in_dim | solution.py:80
  2.1 15.9 %all-to-all-start = ((s32[32,1,128]{2,1,0:T(1,128)}), s32[32,1,128]{2,1,0:T(1,128)S(1)}, u32[]{:S(2)}, u32[]{:S(2)}) async-start(s32[32,1,128]{2,1,0:T(1,128)} %broadcast_in_dim.24), calls=%async_computation | async-start | bytes 32768 | tf_op jit(solution)/shard_map/all_to_all | solution.py:79
  18.0 2.9 %collective-permute-start.3 = (bf16[224,128]{1,0:T(8,128)(2,1)}, bf16[224,128]{1,0:T(8,128)(2,1)S(1)}, u32[]{:S(2)}, u32[]{:S(2)}) collective-permute-start(bf16[224,128]{1,0:T(8,128)(2,1)} %bitcast.49), channel_id=1, source_target_pairs={{0,32},{1,33},{2,34},{3,35},{4,36},{5,37},{6,38},{7,39},{8,40},{9,... | collective-permute-start | bytes 172040 | tf_op jit(solution)/shard_map/ppermute | solution.py:31
  21.0 0.1 pad_add_fusion
  21.0 0.9 collective-permute-done.3
  21.9 0.8 broadcast_select_fusion.3
  22.8 7.9 %collective-permute-start.5 = (bf16[448,128]{1,0:T(8,128)(2,1)S(1)}, bf16[448,128]{1,0:T(8,128)(2,1)S(1)}, u32[]{:S(2)}, u32[]{:S(2)}) collective-permute-start(bf16[448,128]{1,0:T(8,128)(2,1)S(1)} %pad_maximum_fusion.1), channel_id=1, source_target_pairs={{0,0},{1,64},{2,4},{3,68},{4,256},{5,320},{6,260},{7,324},{8,8},{9... | collective-permute-start | bytes 344072 | tf_op jit(solution)/shard_map/ppermute | solution.py:31
  30.7 6.8 %collective-permute-start.4 = (bf16[448,128]{1,0:T(8,128)(2,1)S(1)}, bf16[448,128]{1,0:T(8,128)(2,1)S(1)}, u32[]{:S(2)}, u32[]{:S(2)}) collective-permute-start(bf16[448,128]{1,0:T(8,128)(2,1)S(1)} %pad_maximum_fusion.1), channel_id=1, source_target_pairs={{0,132},{1,196},{2,128},{3,192},{4,388},{5,452},{6,384},{7,448},{8... | collective-permute-start | bytes 344072 | tf_op jit(solution)/shard_map/ppermute | solution.py:31
  37.6 0.6 gather_fusion
  38.2 0.1 convolution_convert_fusion.3
  38.4 1.2 select_reduce_fusion
  39.5 0.1 reshape.374
  39.6 2.7 %gather_fusion.1 = bf16[512,896]{1,0:T(8,128)(2,1)} fusion(bf16[1188,896]{1,0:T(8,128)(2,1)S(1)} %copy-done, s32[1024]{0:T(1024)S(1)} %pad_clamp_fusion), kind=kCustom, calls=%fused_computation.1 | custom fusion | bytes 1837056 | tf_op jit(solution)/shard_map/jit(_take)/gather | solution.py:105
  42.4 10.8 %all-to-all-start.1 = ((bf16[32,16,896]{2,1,0:T(8,128)(2,1)}), bf16[32,16,896]{2,1,0:T(8,128)(2,1)S(1)}, u32[]{:S(2)}, u32[]{:S(2)}) async-start(bf16[32,16,896]{2,1,0:T(8,128)(2,1)} %bitcast.4), calls=%async_computation.1 | async-start | bytes 1835008 | tf_op jit(solution)/shard_map/all_to_all | solution.py:106
  53.3 0.2 convert_reduce_fusion
  53.5 1.4 %convolution_convert_fusion.1 = bf16[512,896]{1,0:T(8,128)(2,1)} fusion(bf16[448,128]{1,0:T(8,128)(2,1)S(1)} %get-tuple-element.13, bf16[448,128]{1,0:T(8,128)(2,1)S(1)} %get-tuple-element.12, s32[128]{0:T(128)S(1)} %and_select_fusion.2), kind=kOutput, calls=%fused_computation.4 | convolution fusion | flops 118489088 | bytes 1147392 | tf_op jit(solution)/shard_map/dot_general | solution.py:136
  54.9 13.2 %all-to-all-done.1 = bf16[32,16,896]{2,1,0:T(8,128)(2,1)S(1)} async-done(((bf16[32,16,896]{2,1,0:T(8,128)(2,1)}), bf16[32,16,896]{2,1,0:T(8,128)(2,1)S(1)}, u32[]{:S(2)}, u32[]{:S(2)}) %all-to-all-start.1) | async-done | bytes 917536 | tf_op jit(solution)/shard_map/all_to_all | solution.py:106
  68.1 5.3 %all-to-all-start.2 = ((bf16[32,16,896]{2,1,0:T(8,128)(2,1)}), bf16[32,16,896]{2,1,0:T(8,128)(2,1)}, u32[]{:S(2)}, u32[]{:S(2)}) async-start(bf16[32,16,896]{2,1,0:T(8,128)(2,1)} %bitcast.15), calls=%async_computation.2 | async-start | bytes 1835008 | tf_op jit(solution)/shard_map/all_to_all | solution.py:139
  73.4 0.2 convert_reduce_fusion.1
  73.6 0.4 convolution_convert_fusion.2
  74.0 1.9 %collective-permute-start.1 = (bf16[128,896]{1,0:T(8,128)(2,1)S(1)}, bf16[128,896]{1,0:T(8,128)(2,1)S(1)}, u32[]{:S(2)}, u32[]{:S(2)}) collective-permute-start(bf16[128,896]{1,0:T(8,128)(2,1)S(1)} %convolution_convert_fusion.2), channel_id=1, source_target_pairs={{0,256},{1,257},{2,258},{3,259},{4,260},{5,261},{6,262},{7,263},{8... | collective-permute-start | bytes 688136 | tf_op jit(solution)/shard_map/ppermute | solution.py:31
  75.9 4.9 %collective-permute-start = (bf16[128,896]{1,0:T(8,128)(2,1)S(1)}, bf16[128,896]{1,0:T(8,128)(2,1)S(1)}, u32[]{:S(2)}, u32[]{:S(2)}) collective-permute-start(bf16[128,896]{1,0:T(8,128)(2,1)S(1)} %convolution_convert_fusion.2), channel_id=1, source_target_pairs={{0,0},{1,1},{2,2},{3,3},{4,4},{5,5},{6,6},{7,7},{8,8},{9,9},{10,10... | collective-permute-start | bytes 688136 | tf_op jit(solution)/shard_map/ppermute | solution.py:31
  80.9 0.1 eq.171
  80.9 13.9 %collective-permute-done.1 = bf16[128,896]{1,0:T(8,128)(2,1)S(1)} collective-permute-done((bf16[128,896]{1,0:T(8,128)(2,1)S(1)}, bf16[128,896]{1,0:T(8,128)(2,1)S(1)}, u32[]{:S(2)}, u32[]{:S(2)}) %collective-permute-start.1) | collective-permute-done | bytes 229408 | tf_op jit(solution)/shard_map/ppermute | solution.py:31
  94.8 6.6 %collective-permute-done = bf16[128,896]{1,0:T(8,128)(2,1)S(1)} collective-permute-done((bf16[128,896]{1,0:T(8,128)(2,1)S(1)}, bf16[128,896]{1,0:T(8,128)(2,1)S(1)}, u32[]{:S(2)}, u32[]{:S(2)}) %collective-permute-start) | collective-permute-done | bytes 229408 | tf_op jit(solution)/shard_map/ppermute | solution.py:31
  101.4 0.1 add.330
  101.5 5.7 %collective-permute-start.2 = (bf16[128,896]{1,0:T(8,128)(2,1)S(1)}, bf16[128,896]{1,0:T(8,128)(2,1)S(1)}, u32[]{:S(2)}, u32[]{:S(2)}) collective-permute-start(bf16[128,896]{1,0:T(8,128)(2,1)S(1)} %add.330), channel_id=1, source_target_pairs={{0,32},{32,0},{1,33},{33,1},{2,34},{34,2},{3,35},{35,3},{4,36},{36... | collective-permute-start | bytes 688136 | tf_op jit(solution)/shard_map/ppermute | solution.py:120
  107.2 3.9 %convolution_convert_fusion = bf16[1188,896]{1,0:T(8,128)(2,1)} fusion(bf16[512,896]{1,0:T(8,128)(2,1)} %bitcast.16, s32[512]{0:T(512)S(1)} %eq.171), kind=kOutput, calls=%fused_computation.2 | convolution fusion | flops 1091667456 | bytes 3048448 | tf_op jit(solution)/shard_map/dot_general | solution.py:142
  111.2 0.1 add.331
  111.2 12.7 %all-gather = bf16[512,896]{1,0:T(8,128)(2,1)S(1)} all-gather(bf16[128,896]{1,0:T(8,128)(2,1)S(1)} %add.331), channel_id=2, replica_groups=mesh['z_hi'=2,'y'=4,'core'=2,'x'=4,'z_lo'=8] {'y'}, dimensions={0}, use_global_device_ids=true | all-gather | bytes 1146880 | tf_op jit(solution)/shard_map/all_gather | solution.py:121
  123.9 0.1 dynamic-slice_bitcast_fusion.3
  124.0 1.0 pad_maximum_fusion
  (19 shorter events, 0.2 us)
Async XLA Ops:
  0.6 39.0 %copy-start = (bf16[1188,896]{1,0:T(8,128)(2,1)S(1)}, bf16[1188,896]{1,0:T(8,128)(2,1)}, u32[]{:S(2)}) copy-start(bf16[1188,896]{1,0:T(8,128)(2,1)} %param.4) | copy-start | bytes 6386692
  2.1 35.5 %all-to-all-start = ((s32[32,1,128]{2,1,0:T(1,128)}), s32[32,1,128]{2,1,0:T(1,128)S(1)}, u32[]{:S(2)}, u32[]{:S(2)}) async-start(s32[32,1,128]{2,1,0:T(1,128)} %broadcast_in_dim.24), calls=%async_computation | async-start | bytes 32768 | tf_op jit(solution)/shard_map/all_to_all | solution.py:79
  18.0 4.0 %collective-permute-start.3 = (bf16[224,128]{1,0:T(8,128)(2,1)}, bf16[224,128]{1,0:T(8,128)(2,1)S(1)}, u32[]{:S(2)}, u32[]{:S(2)}) collective-permute-start(bf16[224,128]{1,0:T(8,128)(2,1)} %bitcast.49), channel_id=1, source_target_pairs={{0,32},{1,33},{2,34},{3,35},{4,36},{5,37},{6,38},{7,39},{8,40},{9,... | collective-permute-start | bytes 172040 | tf_op jit(solution)/shard_map/ppermute | solution.py:31
  22.8 30.7 %collective-permute-start.5 = (bf16[448,128]{1,0:T(8,128)(2,1)S(1)}, bf16[448,128]{1,0:T(8,128)(2,1)S(1)}, u32[]{:S(2)}, u32[]{:S(2)}) collective-permute-start(bf16[448,128]{1,0:T(8,128)(2,1)S(1)} %pad_maximum_fusion.1), channel_id=1, source_target_pairs={{0,0},{1,64},{2,4},{3,68},{4,256},{5,320},{6,260},{7,324},{8,8},{9... | collective-permute-start | bytes 344072 | tf_op jit(solution)/shard_map/ppermute | solution.py:31
  30.7 22.7 %collective-permute-start.4 = (bf16[448,128]{1,0:T(8,128)(2,1)S(1)}, bf16[448,128]{1,0:T(8,128)(2,1)S(1)}, u32[]{:S(2)}, u32[]{:S(2)}) collective-permute-start(bf16[448,128]{1,0:T(8,128)(2,1)S(1)} %pad_maximum_fusion.1), channel_id=1, source_target_pairs={{0,132},{1,196},{2,128},{3,192},{4,388},{5,452},{6,384},{7,448},{8... | collective-permute-start | bytes 344072 | tf_op jit(solution)/shard_map/ppermute | solution.py:31
  42.4 25.7 %all-to-all-start.1 = ((bf16[32,16,896]{2,1,0:T(8,128)(2,1)}), bf16[32,16,896]{2,1,0:T(8,128)(2,1)S(1)}, u32[]{:S(2)}, u32[]{:S(2)}) async-start(bf16[32,16,896]{2,1,0:T(8,128)(2,1)} %bitcast.4), calls=%async_computation.1 | async-start | bytes 1835008 | tf_op jit(solution)/shard_map/all_to_all | solution.py:106
  68.1 39.1 %all-to-all-start.2 = ((bf16[32,16,896]{2,1,0:T(8,128)(2,1)}), bf16[32,16,896]{2,1,0:T(8,128)(2,1)}, u32[]{:S(2)}, u32[]{:S(2)}) async-start(bf16[32,16,896]{2,1,0:T(8,128)(2,1)} %bitcast.15), calls=%async_computation.2 | async-start | bytes 1835008 | tf_op jit(solution)/shard_map/all_to_all | solution.py:139
  74.0 20.8 %collective-permute-start.1 = (bf16[128,896]{1,0:T(8,128)(2,1)S(1)}, bf16[128,896]{1,0:T(8,128)(2,1)S(1)}, u32[]{:S(2)}, u32[]{:S(2)}) collective-permute-start(bf16[128,896]{1,0:T(8,128)(2,1)S(1)} %convolution_convert_fusion.2), channel_id=1, source_target_pairs={{0,256},{1,257},{2,258},{3,259},{4,260},{5,261},{6,262},{7,263},{8... | collective-permute-start | bytes 688136 | tf_op jit(solution)/shard_map/ppermute | solution.py:31
  75.9 25.5 %collective-permute-start = (bf16[128,896]{1,0:T(8,128)(2,1)S(1)}, bf16[128,896]{1,0:T(8,128)(2,1)S(1)}, u32[]{:S(2)}, u32[]{:S(2)}) collective-permute-start(bf16[128,896]{1,0:T(8,128)(2,1)S(1)} %convolution_convert_fusion.2), channel_id=1, source_target_pairs={{0,0},{1,1},{2,2},{3,3},{4,4},{5,5},{6,6},{7,7},{8,8},{9,9},{10,10... | collective-permute-start | bytes 688136 | tf_op jit(solution)/shard_map/ppermute | solution.py:31
  101.5 9.7 %collective-permute-start.2 = (bf16[128,896]{1,0:T(8,128)(2,1)S(1)}, bf16[128,896]{1,0:T(8,128)(2,1)S(1)}, u32[]{:S(2)}, u32[]{:S(2)}) collective-permute-start(bf16[128,896]{1,0:T(8,128)(2,1)S(1)} %add.330), channel_id=1, source_target_pairs={{0,32},{32,0},{1,33},{33,1},{2,34},{34,2},{3,35},{35,3},{4,36},{36... | collective-permute-start | bytes 688136 | tf_op jit(solution)/shard_map/ppermute | solution.py:120

commit v4 on v3

--- a/solution.py
+++ b/solution.py
@@ -29,6 +29,10 @@
         for place in itertools.product(*(range(size) for size in SIZES))
     ]
     return lax.ppermute(values, NAMES, pairs)
+
+
+def lookup_code(z_hi, z_lo):
+    return z_lo ^ (z_hi * 4)
 
 
 def grad_code(z_hi, z_lo):
@@ -88,10 +92,9 @@
     late = move(half, functools.partial(grad_target, 1))
     sent = (early, late)
 
-    code_f = z_lo
+    code_f = lookup_code(z_hi, z_lo)
     code_b = grad_code(z_hi, z_lo)
-    orders = jnp.concatenate([groups_of_plane(code_f), groups_of_plane(code_b)])
-    ids = jnp.take(every_id, orders, axis=0, mode="clip")
+    ids = jnp.take(every_id, groups_of_plane(code_f), axis=0, mode="clip")
     local = ids - segment * section
     owned = (local >= 0) & (local < section) & (local % PACK == residue)
     line = local // PACK
@@ -102,7 +105,7 @@
     hit = owned[:, None, :] & (rank[:, None, :] == slots[None, :, None])
     row_of = jnp.sum(jnp.where(hit, line[:, None, :] + 1, 0), axis=2) - 1
 
-    fetched = jnp.take(table, jnp.maximum(row_of[:32], 0).reshape(-1), axis=0, mode="clip")
+    fetched = jnp.take(table, jnp.maximum(row_of, 0).reshape(-1), axis=0, mode="clip")
     arrived = lax.all_to_all(fetched.reshape(32, SLOTS, width), PLANE, 0, 0, tiled=True)
     ids_f = lax.dynamic_index_in_dim(every_id, x * 8 + (place ^ code_f), 0, keepdims=False)
     pick_f = pick_matrix(ids_f, section, z_hi, parity)
@@ -111,10 +114,10 @@
     ).astype(BF16)
 
     def near(a, b, c, d, e):
-        return (a, b, c, d, e ^ (c * 4 + b))
+        return (a, b, c, d, lookup_code(a, e) ^ (c * 4 + b))
 
     def far(a, b, c, d, e):
-        return (1 - a, b, c, d, e ^ (c * 4 + b))
+        return (1 - a, b, c, d, lookup_code(a, e) ^ (c * 4 + b))
 
     both = move(picked, near) + move(picked, far)
     quarter = both + lax.ppermute(both, "core", [(0, 1), (1, 0)])
@@ -136,8 +139,17 @@
     packed = lax.dot_general(
         pick_b, piece, (((0,), (1,)), ((), ())), preferred_element_type=jnp.float32
     ).astype(BF16)
+    late_id, packed = lax.optimization_barrier((every_id.reshape(-1), packed))
     returned = lax.all_to_all(packed.reshape(32, SLOTS, width), PLANE, 0, 0, tiled=True)
-    target = row_of[32:].reshape(-1)
+    late_local = late_id - segment * section
+    late_owned = (late_local >= 0) & (late_local < section) & (late_local % PACK == residue)
+    late_line = jnp.where(late_owned, late_local // PACK + 1, 0).reshape(32, tokens)
+    late_line = jnp.take(late_line, groups_of_plane(code_b), axis=0, mode="clip")
+    late_rank = jnp.dot(
+        (late_line > 0).astype(BF16), before, preferred_element_type=jnp.float32
+    ).astype(jnp.int32)
+    late_hit = late_rank[:, None, :] == slots[None, :, None]
+    target = jnp.sum(jnp.where(late_hit, late_line[:, None, :], 0), axis=2).reshape(-1) - 1
     spread = (jnp.arange(lines, dtype=jnp.int32)[:, None] == target[None, :]).astype(BF16)
     table_grad = jnp.dot(
         spread, returned.reshape(32 * SLOTS, width), preferred_element_type=jnp.float32

time: 127 us -> 126 us (level)
  starting transfers between devices: 62.2 us -> 58.4 us
  waiting for transfers between devices: 34.6 us -> 36.5 us
    ppermute x1, starting transfers between devices: 5.72 us -> 1.92 us  [body(): quarter = both + lax.ppermute(both, 'core', [(0, 1), (1, 0)])]
    ppermute x5, waiting for transfers between devices: 21.4 us -> 23.2 us  [move(): return lax.ppermute(values, NAMES, pairs)]
    gather x2 -> x3, local copies, waits for them, and re-layouts: 3.33 us -> 3.89 us  [the longest x1 2.74 us: body(): jnp.take(table, jnp.maximum(row_of, 0).reshape(-1), axis=0, mode='clip')]
  transfers between devices with their start and end apart: 9 -> 9, of which waited for: 4 -> 3; matrix products, arithmetic and copies ran while one was open for 10% -> 10% of each run, Pallas kernels for 0% -> 0%
where the time goes in v4:
time: 126 us; the launch traced here: 125 us
  starting transfers between devices  58.4 us (46%)
  waiting for transfers between devices  36.5 us (29%)
  blocking collectives  13.3 us (11%)
  matrix products  5.99 us (5%)
  local copies, waits for them, and re-layouts  5.55 us (4%)
  other arithmetic  3.74 us (3%)
    ppermute x5, starting transfers between devices, move(): return lax.ppermute(values, NAMES, pairs)  24.4 us
    ppermute x5, waiting for transfers between devices, move(): return lax.ppermute(values, NAMES, pairs)  23.2 us
    all_to_all x1, starting transfers between devices, body(): lax.all_to_all(jnp.broadcast_to(token_ids[None], (32, tokens)), GROUPS, 0...  15.9 us
    all_to_all x1, waiting for transfers between devices, body(): lax.all_to_all(fetched.reshape(32, SLOTS, width), PLANE, 0, 0, tiled=True)  13.4 us
    all_gather x1, blocking collectives, body(): whole = lax.all_gather(quarter, 'y')  13.3 us
    all_to_all x1, starting transfers between devices, body(): lax.all_to_all(fetched.reshape(32, SLOTS, width), PLANE, 0, 0, tiled=True)  10.8 us
    all_to_all x1, starting transfers between devices, body(): lax.all_to_all(packed.reshape(32, SLOTS, width), PLANE, 0, 0, tiled=True)  5.33 us
    dot_general x1, matrix products, body(): jnp.dot(spread, returned.reshape(32 * SLOTS, width), preferred_element_ty...  3.94 us
  transfers between devices with their start and end apart: 9, of which 3 were waited for; matrix products, arithmetic and copies ran while one was open for 10% of the time, Pallas kernels for 0%

profile of v4, /device:TPU:1, one launch (start us, length us, event | category | flops | bytes accessed | tf_op | source)
XLA Modules:
  0.0 124.5 jit_solution(3720542372405705052)
XLA Ops:
  0.6 1.4 %broadcast_in_dim.29 = s32[32,1,128]{2,1,0:T(1,128)} broadcast(s32[128]{0:T(128)} %param.3), dimensions={2} | broadcast | bytes 16896 | tf_op jit(solution)/shard_map/broadcast_in_dim | solution.py:84
  2.1 15.9 %all-to-all-start = ((s32[32,1,128]{2,1,0:T(1,128)}), s32[32,1,128]{2,1,0:T(1,128)S(1)}, u32[]{:S(2)}, u32[]{:S(2)}) async-start(s32[32,1,128]{2,1,0:T(1,128)} %broadcast_in_dim.29), calls=%async_computation | async-start | bytes 32768 | tf_op jit(solution)/shard_map/all_to_all | solution.py:83
  18.0 2.9 %collective-permute-start.3 = (bf16[224,128]{1,0:T(8,128)(2,1)}, bf16[224,128]{1,0:T(8,128)(2,1)S(1)}, u32[]{:S(2)}, u32[]{:S(2)}) collective-permute-start(bf16[224,128]{1,0:T(8,128)(2,1)} %bitcast.57), channel_id=1, source_target_pairs={{0,32},{1,33},{2,34},{3,35},{4,36},{5,37},{6,38},{7,39},{8,40},{9,... | collective-permute-start | bytes 172040 | tf_op jit(solution)/shard_map/ppermute | solution.py:31
  21.1 0.9 collective-permute-done.3
  21.9 0.8 broadcast_select_fusion.3
  22.8 7.9 %collective-permute-start.5 = (bf16[448,128]{1,0:T(8,128)(2,1)S(1)}, bf16[448,128]{1,0:T(8,128)(2,1)S(1)}, u32[]{:S(2)}, u32[]{:S(2)}) collective-permute-start(bf16[448,128]{1,0:T(8,128)(2,1)S(1)} %pad_maximum_fusion.1), channel_id=1, source_target_pairs={{0,0},{1,64},{2,4},{3,68},{4,256},{5,320},{6,260},{7,324},{8,8},{9... | collective-permute-start | bytes 344072 | tf_op jit(solution)/shard_map/ppermute | solution.py:31
  30.7 6.8 %collective-permute-start.4 = (bf16[448,128]{1,0:T(8,128)(2,1)S(1)}, bf16[448,128]{1,0:T(8,128)(2,1)S(1)}, u32[]{:S(2)}, u32[]{:S(2)}) collective-permute-start(bf16[448,128]{1,0:T(8,128)(2,1)S(1)} %pad_maximum_fusion.1), channel_id=1, source_target_pairs={{0,132},{1,196},{2,128},{3,192},{4,388},{5,452},{6,384},{7,448},{8... | collective-permute-start | bytes 344072 | tf_op jit(solution)/shard_map/ppermute | solution.py:31
  37.6 0.2 convert_reduce_fusion
  37.8 0.2 convert_reduce_fusion.1
  37.9 0.6 gather_fusion
  38.6 0.1 convolution_convert_fusion.4
  38.7 0.6 select_reduce_fusion.1
  39.4 0.1 reshape.537
  39.5 2.7 %gather_fusion.1 = bf16[512,896]{1,0:T(8,128)(2,1)} fusion(bf16[1188,896]{1,0:T(8,128)(2,1)S(1)} %copy-done, s32[1024]{0:T(1024)S(1)} %pad_clamp_fusion.1), kind=kCustom, calls=%fused_computation.1 | custom fusion | bytes 1837056 | tf_op jit(solution)/shard_map/jit(_take)/gather | solution.py:108
  42.2 10.8 %all-to-all-start.1 = ((bf16[32,16,896]{2,1,0:T(8,128)(2,1)}), bf16[32,16,896]{2,1,0:T(8,128)(2,1)S(1)}, u32[]{:S(2)}, u32[]{:S(2)}) async-start(bf16[32,16,896]{2,1,0:T(8,128)(2,1)} %bitcast.5), calls=%async_computation.1 | async-start | bytes 1835008 | tf_op jit(solution)/shard_map/all_to_all | solution.py:109
  53.1 1.4 %convolution_convert_fusion.1 = bf16[512,896]{1,0:T(8,128)(2,1)} fusion(bf16[448,128]{1,0:T(8,128)(2,1)S(1)} %get-tuple-element.17, bf16[448,128]{1,0:T(8,128)(2,1)S(1)} %get-tuple-element.16, s32[128]{0:T(128)S(1)} %and_select_fusion.2), kind=kOutput, calls=%fused_computation.5 | convolution fusion | flops 118489088 | bytes 1147392 | tf_op jit(solution)/shard_map/dot_general | solution.py:139
  54.5 13.4 %all-to-all-done.1 = bf16[32,16,896]{2,1,0:T(8,128)(2,1)S(1)} async-done(((bf16[32,16,896]{2,1,0:T(8,128)(2,1)}), bf16[32,16,896]{2,1,0:T(8,128)(2,1)S(1)}, u32[]{:S(2)}, u32[]{:S(2)}) %all-to-all-start.1) | async-done | bytes 917536 | tf_op jit(solution)/shard_map/all_to_all | solution.py:109
  67.9 5.3 %all-to-all-start.2 = ((bf16[32,16,896]{2,1,0:T(8,128)(2,1)}), bf16[32,16,896]{2,1,0:T(8,128)(2,1)}, u32[]{:S(2)}, u32[]{:S(2)}) async-start(bf16[32,16,896]{2,1,0:T(8,128)(2,1)} %bitcast.19), calls=%async_computation.2 | async-start | bytes 1835008 | tf_op jit(solution)/shard_map/all_to_all | solution.py:143
  73.3 0.6 gather_fusion.2
  73.8 0.1 convolution_convert_fusion.3
  74.0 0.4 convolution_convert_fusion.2
  74.3 1.9 %collective-permute-start.1 = (bf16[128,896]{1,0:T(8,128)(2,1)S(1)}, bf16[128,896]{1,0:T(8,128)(2,1)S(1)}, u32[]{:S(2)}, u32[]{:S(2)}) collective-permute-start(bf16[128,896]{1,0:T(8,128)(2,1)S(1)} %convolution_convert_fusion.2), channel_id=1, source_target_pairs={{0,256},{1,257},{2,258},{3,259},{4,260},{5,261},{6,262},{7,263},{8... | collective-permute-start | bytes 688136 | tf_op jit(solution)/shard_map/ppermute | solution.py:31
  76.3 4.9 %collective-permute-start = (bf16[128,896]{1,0:T(8,128)(2,1)S(1)}, bf16[128,896]{1,0:T(8,128)(2,1)S(1)}, u32[]{:S(2)}, u32[]{:S(2)}) collective-permute-start(bf16[128,896]{1,0:T(8,128)(2,1)S(1)} %convolution_convert_fusion.2), channel_id=1, source_target_pairs={{0,0},{1,1},{2,2},{3,3},{4,4},{5,5},{6,6},{7,7},{8,8},{9,9},{10,10... | collective-permute-start | bytes 688136 | tf_op jit(solution)/shard_map/ppermute | solution.py:31
  81.2 0.6 select_reduce_fusion
  81.8 0.1 sub.112
  81.9 22.3 %collective-permute-done.1 = bf16[128,896]{1,0:T(8,128)(2,1)S(1)} collective-permute-done((bf16[128,896]{1,0:T(8,128)(2,1)S(1)}, bf16[128,896]{1,0:T(8,128)(2,1)S(1)}, u32[]{:S(2)}, u32[]{:S(2)}) %collective-permute-start.1) | collective-permute-done | bytes 229408 | tf_op jit(solution)/shard_map/ppermute | solution.py:31
  104.2 1.9 %collective-permute-start.2 = (bf16[128,896]{1,0:T(8,128)(2,1)S(1)}, bf16[128,896]{1,0:T(8,128)(2,1)S(1)}, u32[]{:S(2)}, u32[]{:S(2)}) collective-permute-start(bf16[128,896]{1,0:T(8,128)(2,1)S(1)} %add.420), channel_id=1, source_target_pairs={{0,32},{32,0},{1,33},{33,1},{2,34},{34,2},{3,35},{35,3},{4,36},{36... | collective-permute-start | bytes 688136 | tf_op jit(solution)/shard_map/ppermute | solution.py:123
  106.2 3.9 %convolution_convert_fusion = bf16[1188,896]{1,0:T(8,128)(2,1)} fusion(bf16[512,896]{1,0:T(8,128)(2,1)} %bitcast.20, s32[512]{0:T(512)S(1)} %sub.112), kind=kOutput, calls=%fused_computation.3 | convolution fusion | flops 1091667456 | bytes 3048448 | tf_op jit(solution)/shard_map/dot_general | solution.py:154
  110.1 0.1 add.421
  110.2 13.3 %all-gather = bf16[512,896]{1,0:T(8,128)(2,1)S(1)} all-gather(bf16[128,896]{1,0:T(8,128)(2,1)S(1)} %add.421), channel_id=2, replica_groups=mesh['z_hi'=2,'y'=4,'core'=2,'x'=4,'z_lo'=8] {'y'}, dimensions={0}, use_global_device_ids=true | all-gather | bytes 1146880 | tf_op jit(solution)/shard_map/all_gather | solution.py:124
  123.4 0.1 dynamic-slice_bitcast_fusion.3
  123.5 1.0 pad_maximum_fusion
  (24 shorter events, 0.3 us)
Async XLA Ops:
  0.6 38.8 %copy-start = (bf16[1188,896]{1,0:T(8,128)(2,1)S(1)}, bf16[1188,896]{1,0:T(8,128)(2,1)}, u32[]{:S(2)}) copy-start(bf16[1188,896]{1,0:T(8,128)(2,1)} %param.4) | copy-start | bytes 6386692
  2.1 35.5 %all-to-all-start = ((s32[32,1,128]{2,1,0:T(1,128)}), s32[32,1,128]{2,1,0:T(1,128)S(1)}, u32[]{:S(2)}, u32[]{:S(2)}) async-start(s32[32,1,128]{2,1,0:T(1,128)} %broadcast_in_dim.29), calls=%async_computation | async-start | bytes 32768 | tf_op jit(solution)/shard_map/all_to_all | solution.py:83
  18.0 4.0 %collective-permute-start.3 = (bf16[224,128]{1,0:T(8,128)(2,1)}, bf16[224,128]{1,0:T(8,128)(2,1)S(1)}, u32[]{:S(2)}, u32[]{:S(2)}) collective-permute-start(bf16[224,128]{1,0:T(8,128)(2,1)} %bitcast.57), channel_id=1, source_target_pairs={{0,32},{1,33},{2,34},{3,35},{4,36},{5,37},{6,38},{7,39},{8,40},{9,... | collective-permute-start | bytes 172040 | tf_op jit(solution)/shard_map/ppermute | solution.py:31
  22.8 30.3 %collective-permute-start.5 = (bf16[448,128]{1,0:T(8,128)(2,1)S(1)}, bf16[448,128]{1,0:T(8,128)(2,1)S(1)}, u32[]{:S(2)}, u32[]{:S(2)}) collective-permute-start(bf16[448,128]{1,0:T(8,128)(2,1)S(1)} %pad_maximum_fusion.1), channel_id=1, source_target_pairs={{0,0},{1,64},{2,4},{3,68},{4,256},{5,320},{6,260},{7,324},{8,8},{9... | collective-permute-start | bytes 344072 | tf_op jit(solution)/shard_map/ppermute | solution.py:31
  30.7 22.3 %collective-permute-start.4 = (bf16[448,128]{1,0:T(8,128)(2,1)S(1)}, bf16[448,128]{1,0:T(8,128)(2,1)S(1)}, u32[]{:S(2)}, u32[]{:S(2)}) collective-permute-start(bf16[448,128]{1,0:T(8,128)(2,1)S(1)} %pad_maximum_fusion.1), channel_id=1, source_target_pairs={{0,132},{1,196},{2,128},{3,192},{4,388},{5,452},{6,384},{7,448},{8... | collective-permute-start | bytes 344072 | tf_op jit(solution)/shard_map/ppermute | solution.py:31
  42.2 25.7 %all-to-all-start.1 = ((bf16[32,16,896]{2,1,0:T(8,128)(2,1)}), bf16[32,16,896]{2,1,0:T(8,128)(2,1)S(1)}, u32[]{:S(2)}, u32[]{:S(2)}) async-start(bf16[32,16,896]{2,1,0:T(8,128)(2,1)} %bitcast.5), calls=%async_computation.1 | async-start | bytes 1835008 | tf_op jit(solution)/shard_map/all_to_all | solution.py:109
  67.9 38.3 %all-to-all-start.2 = ((bf16[32,16,896]{2,1,0:T(8,128)(2,1)}), bf16[32,16,896]{2,1,0:T(8,128)(2,1)}, u32[]{:S(2)}, u32[]{:S(2)}) async-start(bf16[32,16,896]{2,1,0:T(8,128)(2,1)} %bitcast.19), calls=%async_computation.2 | async-start | bytes 1835008 | tf_op jit(solution)/shard_map/all_to_all | solution.py:143
  74.3 29.8 %collective-permute-start.1 = (bf16[128,896]{1,0:T(8,128)(2,1)S(1)}, bf16[128,896]{1,0:T(8,128)(2,1)S(1)}, u32[]{:S(2)}, u32[]{:S(2)}) collective-permute-start(bf16[128,896]{1,0:T(8,128)(2,1)S(1)} %convolution_convert_fusion.2), channel_id=1, source_target_pairs={{0,256},{1,257},{2,258},{3,259},{4,260},{5,261},{6,262},{7,263},{8... | collective-permute-start | bytes 688136 | tf_op jit(solution)/shard_map/ppermute | solution.py:31
  76.3 27.9 %collective-permute-start = (bf16[128,896]{1,0:T(8,128)(2,1)S(1)}, bf16[128,896]{1,0:T(8,128)(2,1)S(1)}, u32[]{:S(2)}, u32[]{:S(2)}) collective-permute-start(bf16[128,896]{1,0:T(8,128)(2,1)S(1)} %convolution_convert_fusion.2), channel_id=1, source_target_pairs={{0,0},{1,1},{2,2},{3,3},{4,4},{5,5},{6,6},{7,7},{8,8},{9,9},{10,10... | collective-permute-start | bytes 688136 | tf_op jit(solution)/shard_map/ppermute | solution.py:31
  104.2 5.9 %collective-permute-start.2 = (bf16[128,896]{1,0:T(8,128)(2,1)S(1)}, bf16[128,896]{1,0:T(8,128)(2,1)S(1)}, u32[]{:S(2)}, u32[]{:S(2)}) collective-permute-start(bf16[128,896]{1,0:T(8,128)(2,1)S(1)} %add.420), channel_id=1, source_target_pairs={{0,32},{32,0},{1,33},{33,1},{2,34},{34,2},{3,35},{35,3},{4,36},{36... | collective-permute-start | bytes 688136 | tf_op jit(solution)/shard_map/ppermute | solution.py:123
